TPU v7x, 32 devices: a whole 2x2x4 slice. The times are simulated.
32 devices in a mesh: ex: 2 (over x), blk: 16 (over z, y, core).
Axes of the slice: x: 2, y: 2, z: 4, core: 2. Of those that a mesh axis runs over, the one named last changes fastest.
Arguments:
- activations: bfloat16 [256, 28672], P('blk', 'ex'), may hold values from -6 to 6
- out_grads: bfloat16 [256, 8192], P('ex', 'blk'), may hold values from -0.5 to 0.5
- basis_in: bfloat16 [28672, 28672], P('ex', 'blk'), may hold values from -0.03125 to 0.03125
- basis_out: bfloat16 [8192, 4096], P('blk', 'ex'), may hold values from -0.0625 to 0.0625
- example_ids: int32 [256], replicated, may hold values from 0 to 2, as said below
Outputs:
- correction: float32 [4096, 28672], P('ex', 'blk')
Inputs may be any that keep to these rules, and one draw needn't show every extreme that they name: `example_ids`: example ids never fall along the tokens; every example 0 to 1 holds 1 to 192 tokens, and some example exactly 192; the id 2 marks padding tokens after the last example.
All inputs are finite; a program needn't handle non-finite values.
Results may differ from a plain program's by a relative error of at most 0.0029.
Values may be sent and summed in bfloat16 or wider, within the bound.
No kernel may reach another device: no remote copies, remote signals or barrier semaphores. Data moves between devices by JAX's collectives and lax.ppermute only.
A program may use at most 128 MiB of HBM per device.

v0:
```python
import jax
import jax.numpy as jnp
from jax import lax
from jax.sharding import PartitionSpec as P

LEN = 128
MOST = 192


def local(activations, out_grads, basis_in, basis_out, example_ids):
    partial_in = jnp.dot(
        lax.all_gather(activations, "blk", axis=0, tiled=True),
        basis_in,
        preferred_element_type=jnp.float32,
    )
    grads_all = lax.all_gather(out_grads, "ex", axis=0, tiled=True)
    proj_in = lax.psum(partial_in, "ex").astype(jnp.bfloat16)
    partial_out = jnp.dot(grads_all, basis_out, preferred_element_type=jnp.float32)
    proj_out = lax.psum(partial_out, "blk").astype(jnp.bfloat16)
    token_count = example_ids.shape[0]
    example_count = token_count // LEN

    def add_example(example, running):
        offset = jnp.sum((example_ids < example).astype(jnp.int32))
        window_start = jnp.minimum(offset, token_count - MOST)
        window_ids = lax.dynamic_slice_in_dim(example_ids, window_start, MOST, 0)
        chosen = (window_ids == example).astype(proj_out.dtype)
        out_window = lax.dynamic_slice_in_dim(proj_out, window_start, MOST, 0) * chosen[:, None]
        in_window = lax.dynamic_slice_in_dim(proj_in, window_start, MOST, 0)
        example_grad = lax.dot_general(
            out_window, in_window, (((0,), (0,)), ((), ())), preferred_element_type=jnp.float32
        )
        return running + example_grad * example_grad

    initial = jnp.zeros((proj_out.shape[1], proj_in.shape[1]), jnp.float32)
    running = lax.fori_loop(0, example_count, add_example, initial)
    return running / example_count


def solution(mesh):
    return jax.shard_map(
        local,
        mesh=mesh,
        in_specs=(P("blk", "ex"), P("ex", "blk"), P("ex", "blk"), P("blk", "ex"), P()),
        out_specs=P("ex", "blk"),
        check_vma=False,
    )
```

profile of v0, /device:TPU:0, one launch (start us, length us, event | category | flops | bytes accessed | tf_op | source)
XLA Modules:
  0.0 217.8 jit_solution(209475995248208915)
XLA Ops:
  6.5 0.0 copy-start
  6.5 0.0 all-gather.2.cloned.1.call-start
  6.5 0.7 all-gather.2.cloned.1.call-update
  7.3 7.4 %all_gather.6 = bf16[256,512]{1,0:T(8,128)(2,1)S(1)} all-gather(bf16[128,512]{1,0:T(8,128)(2,1)} %param.8), channel_id=1, replica_groups=mesh['ex'=2,'blk'=16] {'ex'}, dimensions={0}, use_global_device_ids=true | all-gather | bytes 393216 | tf_op jit(solution)/shard_map/all_gather | solution.py:16
  14.7 0.0 copy-done
  14.7 2.1 fusion.6
  16.8 90.0 %all-reduce.3 = bf16[256,2048]{1,0:T(8,128)(2,1)S(1)} all-reduce(f32[256,2048]{1,0:T(8,128)} %fusion.6), channel_id=1, replica_groups=mesh['ex'=2,'blk'=16] {'blk'}, use_global_device_ids=true, to_apply=%region_0.0 | all-reduce | flops 524288 | bytes 3145728 | tf_op jit(solution)/shard_map/psum | solution.py:19
  106.7 0.0 copy-start.2
  106.7 0.0 all-gather.2.cloned.1.call-done
  106.8 24.0 %fusion.7 = f32[256,1792]{1,0:T(8,128)} fusion(bf16[256,14336]{1,0:T(8,128)(2,1)} %all-gather.2.cloned.1.call-done, bf16[14336,1792]{1,0:T(8,128)(2,1)} %param.9), kind=kOutput, calls=%fused_computation.11 | convolution fusion | flops 13153337344 | bytes 60555264 | tf_op jit(solution)/shard_map/dot_general | solution.py:11
  130.8 44.7 %all-reduce.2 = bf16[256,1792]{1,0:T(8,128)(2,1)S(1)} all-reduce(f32[256,1792]{1,0:T(8,128)} %fusion.7), channel_id=1, replica_groups=mesh['ex'=2,'blk'=16] {'ex'}, use_global_device_ids=true, to_apply=%region_1.0 | all-reduce | flops 458752 | bytes 2752512 | tf_op jit(solution)/shard_map/psum | solution.py:17
  175.4 0.0 copy-done.2
  175.4 23.7 %while.14 = (s32[]{:T(128)}, f32[2048,1792]{1,0:T(8,128)}, s32[256]{0:T(256)S(1)}, bf16[256,2048]{1,0:T(8,128)(2,1)S(1)}, bf16[256,1792]{1,0:T(8,128)(2,1)S(1)},...) while((s32[]{:T(128)}, f32[2048,1792]{1,0:T(8,128)}, s32[256]{0:T(256)S(1)}, ...), condition=%wide.region_4.0_spmd.clone, body=%wide.region_2.0_spmd.clone.sunk | while | flops 1421870208 | bytes 30839084 | solution.py:36
  175.5 0.7 fusion.17
  176.9 0.1 compare_convert_fusion.3
  177.0 7.8 %select_add_fusion.2 = f32[2048,1792]{1,0:T(8,128)} fusion(f32[2048,1792]{1,0:T(8,128)} %get-tuple-element.169, pred[]{:T(512)S(6)} %compare.3, bf16[256,2048]{1,0:T(8,128)(2,1)S(1)} %get-tuple-element.180, s32[]{:T(128)S(6)} %select_n.11, bf16[256,1792]{1,0:T(8,128)(2,1)S(1)} %get-tuple-element.181, bf16[192]{0:T(256)(128)(2,1)S(1)} %compare_convert_fusion.3), kind=kOutput, calls=%fused_computation.clone.1 | convolution fusion | flops 1421869056 | bytes 30836736 | tf_op jit(solution)/shard_map/while/body/eval_jaxpr/dot_general | solution.py:30
  184.7 0.7 fusion.17
  186.2 0.1 compare_convert_fusion.3
  186.2 12.9 %select_add_fusion.2 = f32[2048,1792]{1,0:T(8,128)} fusion(f32[2048,1792]{1,0:T(8,128)} %get-tuple-element.169, pred[]{:T(512)S(6)} %compare.3, bf16[256,2048]{1,0:T(8,128)(2,1)S(1)} %get-tuple-element.180, s32[]{:T(128)S(6)} %select_n.11, bf16[256,1792]{1,0:T(8,128)(2,1)S(1)} %get-tuple-element.181, bf16[192]{0:T(256)(128)(2,1)S(1)} %compare_convert_fusion.3), kind=kOutput, calls=%fused_computation.clone.1 | convolution fusion | flops 1421869056 | bytes 30836736 | tf_op jit(solution)/shard_map/while/body/eval_jaxpr/dot_general | solution.py:30
  199.2 0.0 copy-start.1
  199.2 11.7 %broadcast_multiply_fusion = f32[2048,1792]{1,0:T(8,128)} fusion(f32[2048,1792]{1,0:T(8,128)} %get-tuple-element.99), kind=kLoop, calls=%fused_computation.9 | loop fusion | flops 3670016 | bytes 29360128 | tf_op jit(solution)/shard_map/div | solution.py:37
  210.9 0.0 copy-done.1
  (1 shorter events, 0.0 us)
Async XLA Ops:
  6.5 8.1 %copy-start = (bf16[512,2048]{1,0:T(8,128)(2,1)S(1)}, bf16[512,2048]{1,0:T(8,128)(2,1)}, u32[]{:S(2)}) copy-start(bf16[512,2048]{1,0:T(8,128)(2,1)} %param.10) | copy-start | bytes 6291460
  6.5 100.2 %all-gather.2.cloned.1.call-start = ((), (), s32[]{:S(2)}) async-start(), calls=%async_computation | async-start | bytes 7798784 | tf_op jit(solution)/shard_map/all_gather | solution.py:12
  106.7 68.7 %copy-start.2 = (s32[256]{0:T(256)S(1)}, s32[256]{0:T(256)}, u32[]{:S(2)}) copy-start(s32[256]{0:T(256)} %param.11) | copy-start | bytes 3076
  199.2 11.7 %copy-start.1 = (bf16[512,2048]{1,0:T(8,128)(2,1)S(1)}, bf16[512,2048]{1,0:T(8,128)(2,1)}, u32[]{:S(2)}) copy-start(bf16[512,2048]{1,0:T(8,128)(2,1)} %param.10) | copy-start | bytes 6291460
Sparse Core Ops, SparseCore 0:
  9.6 94.4 all-gather.1
where the time goes:
time: 218 us
  blocking collectives  142 us (65%)
  matrix products  46.8 us (21%)
  between operations  13.4 us (6%)
  other arithmetic  13.3 us (6%)
    psum x1, blocking collectives, local(): proj_out = lax.psum(partial_out, 'blk').astype(jnp.bfloat16)  90 us
    psum x1, blocking collectives, local(): proj_in = lax.psum(partial_in, 'ex').astype(jnp.bfloat16)  44.7 us
    dot_general x1, matrix products, local(): jnp.dot(lax.all_gather(activations, 'blk', axis=0, tiled=True), basis_in,...  24 us
    dot_general x2, matrix products, add_example(): lax.dot_general(out_window, in_window, (((0,), (0,)), ((), ())), preferre...  20.7 us
    div x1, other arithmetic, local(): return running / example_count  11.7 us
    all_gather x1, blocking collectives, local(): grads_all = lax.all_gather(out_grads, 'ex', axis=0, tiled=True)  7.39 us
  transfers between devices with their start and end apart: 1, of which 0 were waited for; matrix products, arithmetic and copies ran while one was open for 1% of the time, Pallas kernels for 0%

commit v1 on v0

v1 whole, which is shorter than its diff:
```python
import functools

import jax
import jax.numpy as jnp
from jax import lax
from jax.experimental import pallas as pl
from jax.experimental.pallas import tpu as pltpu
from jax.sharding import PartitionSpec as P


LEN = 128
CHUNKS = 2
MIB = 2**20


def tile_of(width, most):
    return most if width % most == 0 else width


def project_out_body(where, *refs):
    *grads, basis, give, keep = refs
    for k, ref in enumerate(grads):
        term = lax.dot_general(
            basis[...], ref[...], (((0,), (1,)), ((), ())), preferred_element_type=jnp.float32
        )
        size = ref.shape[0]
        at = pl.ds(pl.multiple_of(where[1 + k] * size, size), size)

        @pl.when(pl.program_id(0) == 0)
        def _():
            give[:, at] = term

        @pl.when(pl.program_id(0) == 1)
        def _():
            keep[:, at] = term


def project_out(where, grads, basis):
    depth, width = basis.shape
    tokens = sum(g.shape[0] for g in grads)
    half = jax.ShapeDtypeStruct((width // 2, tokens), jnp.float32)
    fixed = lambda i, *_: (0, 0)
    return pl.pallas_call(
        project_out_body,
        grid_spec=pltpu.PrefetchScalarGridSpec(
            num_scalar_prefetch=1,
            grid=(2,),
            in_specs=[pl.BlockSpec(g.shape, fixed) for g in grads]
            + [pl.BlockSpec((depth, width // 2), lambda i, where: (0, (where[0] + 1 + i) % 2))],
            out_specs=[pl.BlockSpec(half.shape, fixed)] * 2,
        ),
        out_shape=[half, half],
        compiler_params=pltpu.CompilerParams(vmem_limit_bytes=12 * MIB),
        cost_estimate=pl.CostEstimate(flops=2 * depth * width * tokens, bytes_accessed=8 * MIB, transcendentals=0),
        name="project_out",
    )(where, *grads, basis)


def project_in_body(pieces, has_start, has_send, *refs):
    parts, refs = refs[:pieces], list(refs[pieces:])
    basis = refs.pop(0)
    start = refs.pop(0) if has_start else None
    packed = refs.pop()

    @pl.when(pl.program_id(0) == 0)
    def _():
        at = 0
        for ref in parts:
            packed[at:at + ref.shape[0], :] = ref[...]
            at += ref.shape[0]

    total = jnp.dot(packed[...], basis[...], preferred_element_type=jnp.float32)
    if has_start:
        total = start[...] + total
    refs[0][...] = total
    if has_send:
        refs[1][...] = total.astype(jnp.bfloat16)


def project_in(parts, basis, chunk, start, send, tile, first, last):
    depth = parts[0].shape[1]
    width = (last - first) * tile
    tokens = sum(p.shape[0] for p in parts)
    shapes = [jax.ShapeDtypeStruct((tokens, width), jnp.float32)]
    if send:
        shapes.append(jax.ShapeDtypeStruct((tokens, width), jnp.bfloat16))
    columns = pl.BlockSpec((tokens, tile), lambda i: (0, i))
    from_start = pl.BlockSpec((tokens, tile), lambda i: (0, first + i))
    return pl.pallas_call(
        functools.partial(project_in_body, len(parts), start is not None, send),
        grid=(width // tile,),
        in_specs=[pl.BlockSpec(p.shape, lambda i: (0, 0)) for p in parts]
        + [pl.BlockSpec((depth, tile), lambda i: (chunk, first + i))]
        + ([from_start] if start is not None else []),
        out_specs=[columns] * len(shapes),
        out_shape=shapes,
        scratch_shapes=[pltpu.VMEM((tokens, depth), jnp.bfloat16)],
        compiler_params=pltpu.CompilerParams(vmem_limit_bytes=28 * MIB),
        cost_estimate=pl.CostEstimate(
            flops=2 * tokens * depth * width, bytes_accessed=2 * depth * width, transcendentals=0
        ),
        name="project_in",
    )(*parts, basis, *([start] if start is not None else []))


def correct_body(examples, blocks, spans, order, rows, *refs):
    *found, ids, pieces, corr, proj, picked = refs
    size = proj.shape[0] // blocks
    count, step, _ = pieces.shape

    @pl.when(pl.program_id(0) == 0)
    def _():
        for t in range(blocks):
            at = pl.ds(t * size, size)
            to = pl.ds(pl.multiple_of(order[t] * size, size), size)
            begin = 0
            for span in range(spans):
                own, *others = found[span::spans]
                total = own[at, :]
                for ref in others:
                    total = total + ref[at, :].astype(jnp.float32)
                end = begin + own.shape[1]
                proj[to, begin:end] = total.astype(jnp.bfloat16)
                begin = end
        for m in range(count):
            piece = pieces[m]
            to = pl.ds(pl.multiple_of(rows[m] * step, step), step)
            for e in range(examples):
                picked[e, to, :] = jnp.where(ids[...] == e, piece, jnp.zeros_like(piece))

    tall = corr.shape[0]
    here = pl.ds(pl.multiple_of(pl.program_id(0) * tall, tall), tall)
    wide = tile_of(corr.shape[1], 256)
    for n in range(corr.shape[1] // wide):
        cols = slice(n * wide, (n + 1) * wide)
        running = None
        for e in range(examples):
            grad = jnp.dot(picked[e, here, :], proj[:, cols], preferred_element_type=jnp.float32)
            running = grad * grad if running is None else running + grad * grad
        corr[:, cols] = running / examples


def correction(order, rows, own, others, pieces, ids, examples, blocks):
    count, step, tokens = pieces.shape
    width = sum(o.shape[1] for o in own)
    whole = lambda m, *_: (0, 0)
    height = count * step
    tall = tile_of(height, 256)
    flops = 2 * examples * height * tokens * width
    return pl.pallas_call(
        functools.partial(correct_body, examples, blocks, len(own)),
        grid_spec=pltpu.PrefetchScalarGridSpec(
            num_scalar_prefetch=2,
            grid=(height // tall,),
            in_specs=[pl.BlockSpec(o.shape, whole) for o in (*own, *others)]
            + [pl.BlockSpec((1, tokens), whole), pl.BlockSpec(pieces.shape, lambda m, *_: (0, 0, 0))],
            out_specs=pl.BlockSpec((tall, width), lambda m, *_: (m, 0)),
            scratch_shapes=[
                pltpu.VMEM((tokens, width), jnp.bfloat16),
                pltpu.VMEM((examples, height, tokens), jnp.bfloat16),
            ],
        ),
        out_shape=jax.ShapeDtypeStruct((height, width), jnp.float32),
        compiler_params=pltpu.CompilerParams(vmem_limit_bytes=28 * MIB),
        cost_estimate=pl.CostEstimate(flops=flops, bytes_accessed=4 * height * width, transcendentals=0),
        name="correction",
    )(order, rows, *own, *others, ids, pieces)


def after(value, *earlier):
    return lax.optimization_barrier((value, *earlier))[0]


def local(parts, blocks, activations, out_grads, basis_in, basis_out, example_ids):
    line = blocks // 4
    me = lax.axis_index("blk")
    z, y, c = me // 4, (me // 2) % 2, me % 2

    def send(x, axis, size, to):
        return lax.ppermute(x, axis, [(i, to(i)) for i in range(size)])

    def core(x):
        return send(x, "blk", blocks, lambda i: i ^ 1)

    def side(x):
        return send(x, "blk", blocks, lambda i: i ^ 2)

    def shift(x, k):
        return send(x, "blk", blocks, lambda i: (i + 4 * k) % blocks)

    depth = activations.shape[1] // CHUNKS
    found = []
    for j in range(CHUNKS):
        own = activations[:, j * depth:(j + 1) * depth]
        rows = [own, side(own)]
        for k in range(1, line):
            far = shift(own, k)
            rows += [far, side(far)]
        found.append(rows)

    mine = lax.axis_index("ex")
    grads = [out_grads]
    for k in range(1, parts):
        grads.append(send(out_grads, "ex", parts, lambda i: (i + k) % parts))
    where = jnp.stack([c] + [(mine - k) % parts for k in range(parts)]).astype(jnp.int32)
    give, total = project_out(where, grads, basis_out)

    def picked(x, count, i):
        return lax.dynamic_index_in_dim(x.reshape(count, x.shape[0] // count, x.shape[1]), i, 0, keepdims=False)

    got = core(give)
    give = picked(total, 2, 1 - y) + picked(got, 2, 1 - y)
    total = picked(total, 2, y) + picked(got, 2, y)
    total = total + side(give)

    tile = tile_of(basis_in.shape[1], 256)
    tiles = basis_in.shape[1] // tile
    cuts = [0, (tiles + 1) // 2, tiles] if tiles > 1 else [0, tiles]
    partial_in = None
    for j in range(CHUNKS):
        rows = found[j]
        if partial_in is not None:
            rows = [after(r, partial_in) for r in rows]
        rows = rows + [core(r) for r in rows]
        if j < CHUNKS - 1:
            partial_in, = project_in(rows, basis_in, j, partial_in, False, tile, 0, tiles)
            if j == 0:
                total = after(total, partial_in)
                gifts = [shift(picked(total, line, (z + k) % line), k) for k in range(1, line)]
        else:
            sums = []
            for first, last in zip(cuts, cuts[1:]):
                sums.append(project_in(rows, basis_in, j, partial_in, parts == 2, tile, first, last))
    total = picked(after(total, sums[0][0]), line, z)
    for gift in gifts:
        total = total + gift
    piece = total.astype(jnp.bfloat16)
    out_line = jnp.stack([piece] + [shift(piece, k) for k in range(1, line)])
    out_side = jnp.concatenate([out_line, side(out_line)])
    proj_out = jnp.concatenate([out_side, core(out_side)])
    at = jnp.arange(blocks, dtype=jnp.int32)
    rows = (c ^ (at // (2 * line))) * (2 * line) + (y ^ (at // line % 2)) * line + (z - at % line) % line
    order = ((z - at % (2 * line) // 2) % line * 2 + (y ^ (at % 2))) * 2 + (c ^ (at // (2 * line)))

    if parts == 2:
        own = [s[0] for s in sums]
        others = [send(s[1], "ex", parts, lambda i: 1 - i) for s in sums]
    else:
        own = [lax.psum(s[0], "ex") for s in sums]
        others = []
    examples = example_ids.shape[0] // LEN
    return correction(order.astype(jnp.int32), rows.astype(jnp.int32), own, others, proj_out,
                      example_ids[None, :], examples, blocks)


def solution(mesh):
    parts, blocks = mesh.shape["ex"], mesh.shape["blk"]

    def body(*args):
        return local(parts, blocks, *args)

    return jax.shard_map(
        body,
        mesh=mesh,
        in_specs=(P("blk", "ex"), P("ex", "blk"), P("ex", "blk"), P("blk", "ex"), P()),
        out_specs=P("ex", "blk"),
        check_vma=False,
    )
```

time: 218 us -> 178 us (0.82)
  blocking collectives: 142 us -> 0 us
  waiting for transfers between devices: 0.73 us -> 54.3 us
  starting transfers between devices: 0.01 us -> 48.6 us
  matrix products: 46.8 us -> 0 us
  Pallas kernels: 0 us -> 41.7 us
  local copies, waits for them, and re-layouts: 0.01 us -> 29.2 us
  between operations: 13.4 us -> 0.28 us
  other arithmetic: 13.3 us -> 3.36 us
    psum x2 -> x0, blocking collectives: 135 us -> none  [the longest x1 90 us: local(): proj_out = lax.psum(partial_out, 'blk').astype(jnp.bfloat16)]
    ppermute x0 -> x43, waiting for transfers between devices: none -> 54.3 us  [send(): return lax.ppermute(x, axis, [(i, to(i)) for i in range(size)])]
    ppermute x0 -> x43, starting transfers between devices: none -> 48.6 us  [send(): return lax.ppermute(x, axis, [(i, to(i)) for i in range(size)])]
    dot_general x4 -> x0, matrix products: 46.8 us -> none  [the longest x1 24 us: local(): jnp.dot(lax.all_gather(activations, 'blk', axis=0, tiled=True), basis_in,...]
    pallas_call x0 -> x5, Pallas kernels: none -> 41.7 us  [the longest x3 29 us: project_in(): pl.pallas_call(functools.partial(project_in_body, len(parts), start is no...]
    unnamed x6 -> x74, local copies, waits for them, and re-layouts: 0.01 us -> 28 us
    div x1 -> x0, other arithmetic: 11.7 us -> none  [local(): return running / example_count]
    all_gather x1 -> x0, blocking collectives: 7.39 us -> none  [local(): grads_all = lax.all_gather(out_grads, 'ex', axis=0, tiled=True)]
  transfers between devices with their start and end apart: 1 -> 43, of which waited for: 0 -> 12; matrix products, arithmetic and copies ran while one was open for 1% -> 3% of each run, Pallas kernels for 0% -> 16%
where the time goes in v1:
time: 178 us
  waiting for transfers between devices  54.3 us (31%)
  starting transfers between devices  48.6 us (27%)
  Pallas kernels  41.7 us (23%)
  local copies, waits for them, and re-layouts  29.2 us (16%)
  other arithmetic  3.36 us (2%)
    ppermute x43, waiting for transfers between devices, send(): return lax.ppermute(x, axis, [(i, to(i)) for i in range(size)])  54.3 us
    ppermute x43, starting transfers between devices, send(): return lax.ppermute(x, axis, [(i, to(i)) for i in range(size)])  48.6 us
    pallas_call x3, Pallas kernels, project_in(): pl.pallas_call(functools.partial(project_in_body, len(parts), start is no...  29 us
    unnamed x74, local copies, waits for them, and re-layouts  28 us
    pallas_call x1, Pallas kernels, correction(): pl.pallas_call(functools.partial(correct_body, examples, blocks, len(own)...  8.99 us
    pallas_call x1, Pallas kernels, project_out(): pl.pallas_call(project_out_body, grid_spec=pltpu.PrefetchScalarGridSpec(n...  3.74 us
  transfers between devices with their start and end apart: 43, of which 12 were waited for; matrix products, arithmetic and copies ran while one was open for 3% of the time, Pallas kernels for 16%

profile of v1, /device:TPU:0, one launch (start us, length us, event | category | flops | bytes accessed | tf_op | source)
XLA Modules:
  0.0 177.5 jit_solution(8768779657730709761)
XLA Ops:
  0.0 3.0 %collective-permute-start.32 = (bf16[128,512]{1,0:T(8,128)(2,1)}, bf16[128,512]{1,0:T(8,128)(2,1)S(1)}, u32[]{:S(2)}, u32[]{:S(2)}) collective-permute-start(bf16[128,512]{1,0:T(8,128)(2,1)} %refs_0_.1), channel_id=1, source_target_pairs={{0,16},{16,0},{1,17},{17,1},{2,18},{18,2},{3,19},{19,3},{4,20},{20... | collective-permute-start | bytes 393224 | tf_op jit(solution)/shard_map/ppermute | solution.py:180
  3.0 3.6 %collective-permute-done.32.refs_1_ = bf16[128,512]{1,0:T(8,128)(2,1)S(1)} collective-permute-done((bf16[128,512]{1,0:T(8,128)(2,1)}, bf16[128,512]{1,0:T(8,128)(2,1)S(1)}, u32[]{:S(2)}, u32[]{:S(2)}) %collective-permute-start.32) | collective-permute-done | bytes 131104 | tf_op jit(solution)/shard_map/ppermute | solution.py:180
  6.7 1.6 copy-done
  9.2 3.7 %project_out.1 = (f32[1024,256]{1,0:T(8,128)S(1)}, f32[1024,256]{1,0:T(8,128)S(1)}) custom-call(s32[3]{0:T(128)S(1)} %pad_add_fusion.where, bf16[128,512]{1,0:T(8,128)(2,1)S(1)} %copy-done.32, bf16[128,512]{1,0:T(8,128)(2,1)S(1)} %collective-permute-done.32.refs_1_, bf16[512,2048]{1,0:T(8,128)(2,1)S(1)} %copy-done), custom_call_target="tpu_custom_call" | custom-call | flops 536870912 | bytes 8388608 | tf_op jit(solution)/shard_map/project_out/pallas_call | solution.py:43
  14.1 3.9 %collective-permute-start.20 = (bf16[16,7168]{1,0:T(8,128)(2,1)S(1)}, bf16[16,7168]{1,0:T(8,128)(2,1)S(1)}, u32[]{:S(2)}, u32[]{:S(2)}) collective-permute-start(bf16[16,7168]{1,0:T(8,128)(2,1)S(1)} %get-tuple-element.21.refs_0_), channel_id=1, source_target_pairs={{0,12},{1,13},{2,14},{3,15},{4,0},{5,1},{6,2},{7,3},{8,4},{9,5},{1... | collective-permute-start | bytes 688136 | tf_op jit(solution)/shard_map/ppermute | solution.py:180
  19.0 5.1 %collective-permute-done.20.refs_6_ = bf16[16,7168]{1,0:T(8,128)(2,1)S(1)} collective-permute-done((bf16[16,7168]{1,0:T(8,128)(2,1)S(1)}, bf16[16,7168]{1,0:T(8,128)(2,1)S(1)}, u32[]{:S(2)}, u32[]{:S(2)}) %collective-permute-start.20) | collective-permute-done | bytes 229408 | tf_op jit(solution)/shard_map/ppermute | solution.py:180
  24.1 4.3 %collective-permute-start.5 = (bf16[16,7168]{1,0:T(8,128)(2,1)S(1)}, bf16[16,7168]{1,0:T(8,128)(2,1)S(1)}, u32[]{:S(2)}, u32[]{:S(2)}) collective-permute-start(bf16[16,7168]{1,0:T(8,128)(2,1)S(1)} %get-tuple-element.42.refs_0_), channel_id=1, source_target_pairs={{0,12},{1,13},{2,14},{3,15},{4,0},{5,1},{6,2},{7,3},{8,4},{9,5},{1... | collective-permute-start | bytes 688136 | tf_op jit(solution)/shard_map/ppermute | solution.py:180
  28.4 10.4 %collective-permute-done.18.refs_4_ = bf16[16,7168]{1,0:T(8,128)(2,1)} collective-permute-done((bf16[16,7168]{1,0:T(8,128)(2,1)S(1)}, bf16[16,7168]{1,0:T(8,128)(2,1)}, u32[]{:S(2)}, u32[]{:S(2)}) %collective-permute-start.18) | collective-permute-done | bytes 229408 | tf_op jit(solution)/shard_map/ppermute | solution.py:180
  38.8 10.8 %collective-permute-start.1 = (bf16[16,7168]{1,0:T(8,128)(2,1)S(1)}, bf16[16,7168]{1,0:T(8,128)(2,1)S(1)}, u32[]{:S(2)}, u32[]{:S(2)}) collective-permute-start(bf16[16,7168]{1,0:T(8,128)(2,1)S(1)} %get-tuple-element.42.refs_0_), channel_id=1, source_target_pairs={{0,4},{1,5},{2,6},{3,7},{4,8},{5,9},{6,10},{7,11},{8,12},{9,13},{1... | collective-permute-start | bytes 688136 | tf_op jit(solution)/shard_map/ppermute | solution.py:180
  50.3 1.5 collective-permute-start
  52.6 5.3 %collective-permute-done.3.refs_4_ = bf16[16,7168]{1,0:T(8,128)(2,1)S(1)} collective-permute-done((bf16[16,7168]{1,0:T(8,128)(2,1)S(1)}, bf16[16,7168]{1,0:T(8,128)(2,1)S(1)}, u32[]{:S(2)}, u32[]{:S(2)}) %collective-permute-start.3) | collective-permute-done | bytes 229408 | tf_op jit(solution)/shard_map/ppermute | solution.py:180
  57.9 1.5 collective-permute-start.6
  62.0 1.5 collective-permute-start.2
  63.6 2.8 %collective-permute-done.6.refs_7_ = bf16[16,7168]{1,0:T(8,128)(2,1)S(1)} collective-permute-done((bf16[16,7168]{1,0:T(8,128)(2,1)S(1)}, bf16[16,7168]{1,0:T(8,128)(2,1)S(1)}, u32[]{:S(2)}, u32[]{:S(2)}) %collective-permute-start.6) | collective-permute-done | bytes 229408 | tf_op jit(solution)/shard_map/ppermute | solution.py:180
  68.9 2.3 %collective-permute-done.4.refs_5_ = bf16[16,7168]{1,0:T(8,128)(2,1)S(1)} collective-permute-done((bf16[16,7168]{1,0:T(8,128)(2,1)S(1)}, bf16[16,7168]{1,0:T(8,128)(2,1)S(1)}, u32[]{:S(2)}, u32[]{:S(2)}) %collective-permute-start.4) | collective-permute-done | bytes 229408 | tf_op jit(solution)/shard_map/ppermute | solution.py:180
  71.9 2.9 %collective-permute-done.2.refs_3_ = bf16[16,7168]{1,0:T(8,128)(2,1)S(1)} collective-permute-done((bf16[16,7168]{1,0:T(8,128)(2,1)S(1)}, bf16[16,7168]{1,0:T(8,128)(2,1)S(1)}, u32[]{:S(2)}, u32[]{:S(2)}) %collective-permute-start.2) | collective-permute-done | bytes 229408 | tf_op jit(solution)/shard_map/ppermute | solution.py:180
  77.7 1.9 %add_bitcast_fusion = f32[512,256]{1,0:T(8,128)} fusion(f32[2,512,256]{2,1,0:T(8,128)} %bitcast.44, s32[]{:T(128)S(6)} %select_n.114, f32[2,512,256]{2,1,0:T(8,128)S(1)} %bitcast.39), kind=kLoop, calls=%fused_computation.1 | loop fusion | flops 131072 | bytes 1572868 | tf_op jit(solution)/shard_map/add | solution.py:212
  80.3 1.5 collective-permute-start.15
  83.8 1.5 collective-permute-start.19
  85.8 1.5 collective-permute-start.34
  100.5 13.2 %project_in.3.refs_17_ = f32[256,1792]{1,0:T(8,128)S(1)} custom-call(bf16[16,7168]{1,0:T(8,128)(2,1)S(1)} %copy-done.5, bf16[16,7168]{1,0:T(8,128)(2,1)S(1)} %copy-done.15, bf16[16,7168]{1,0:T(8,128)(2,1)S(1)} %copy-done.13, bf16[16,7168]{1,0:T(8,128)(2,1)S(1)} %copy-done.25, bf16[16,7168]{1,0:T(8,128)(2,1)S(1)} %copy-done.11, ...), custom_call_target="tpu_custom_call" | custom-call | flops 6576668672 | bytes 25690112 | tf_op jit(solution)/shard_map/project_in/pallas_call | solution.py:89
  118.8 3.8 %collective-permute-start.37 = (f32[128,256]{1,0:T(8,128)S(1)}, f32[128,256]{1,0:T(8,128)S(1)}, u32[]{:S(2)}, u32[]{:S(2)}) collective-permute-start(f32[128,256]{1,0:T(8,128)S(1)} %get-tuple-element.40), channel_id=1, source_target_pairs={{0,12},{1,13},{2,14},{3,15},{4,0},{5,1},{6,2},{7,3},{8,4},{9,5},{1... | collective-permute-start | bytes 393224 | tf_op jit(solution)/shard_map/ppermute | solution.py:180
  123.5 8.6 %project_in.4 = (f32[256,1024]{1,0:T(8,128)S(1)}, bf16[256,1024]{1,0:T(8,128)(2,1)S(1)}) custom-call(bf16[16,7168]{1,0:T(8,128)(2,1)S(1)} %get-tuple-element.21.refs_0_, bf16[16,7168]{1,0:T(8,128)(2,1)} %collective-permute-done.15.refs_1_, bf16[16,7168]{1,0:T(8,128)(2,1)} %collective-permute-done.16.refs_2_, ...), custom_call_target="tpu_custom_call" | custom-call | flops 3758096384 | bytes 14680064 | tf_op jit(solution)/shard_map/project_in/pallas_call | solution.py:89
  132.1 1.6 collective-permute-start.30
  134.7 2.1 %collective-permute-start.39 = (bf16[128,256]{1,0:T(8,128)(2,1)S(1)}, bf16[128,256]{1,0:T(8,128)(2,1)S(1)}, u32[]{:S(2)}, u32[]{:S(2)}) collective-permute-start(bf16[128,256]{1,0:T(8,128)(2,1)S(1)} %get-tuple-element.38), channel_id=1, source_target_pairs={{0,8},{1,9},{2,10},{3,11},{4,12},{5,13},{6,14},{7,15},{8,0},{9,1},... | collective-permute-start | bytes 196616 | tf_op jit(solution)/shard_map/ppermute | solution.py:180
  136.8 1.9 %collective-permute-start.38 = (bf16[128,256]{1,0:T(8,128)(2,1)S(1)}, bf16[128,256]{1,0:T(8,128)(2,1)S(1)}, u32[]{:S(2)}, u32[]{:S(2)}) collective-permute-start(bf16[128,256]{1,0:T(8,128)(2,1)S(1)} %get-tuple-element.38), channel_id=1, source_target_pairs={{0,4},{1,5},{2,6},{3,7},{4,8},{5,9},{6,10},{7,11},{8,12},{9,13},{1... | collective-permute-start | bytes 196616 | tf_op jit(solution)/shard_map/ppermute | solution.py:180
  138.8 1.8 %collective-permute-done.39 = bf16[128,256]{1,0:T(8,128)(2,1)S(1)} collective-permute-done((bf16[128,256]{1,0:T(8,128)(2,1)S(1)}, bf16[128,256]{1,0:T(8,128)(2,1)S(1)}, u32[]{:S(2)}, u32[]{:S(2)}) %collective-permute-start.39) | collective-permute-done | bytes 65568 | tf_op jit(solution)/shard_map/ppermute | solution.py:180
  140.6 2.2 %collective-permute-done.38 = bf16[128,256]{1,0:T(8,128)(2,1)S(1)} collective-permute-done((bf16[128,256]{1,0:T(8,128)(2,1)S(1)}, bf16[128,256]{1,0:T(8,128)(2,1)S(1)}, u32[]{:S(2)}, u32[]{:S(2)}) %collective-permute-start.38) | collective-permute-done | bytes 65568 | tf_op jit(solution)/shard_map/ppermute | solution.py:180
  143.5 6.1 %collective-permute-done.41 = bf16[4,128,256]{2,1,0:T(8,128)(2,1)S(1)} collective-permute-done((bf16[4,128,256]{2,1,0:T(8,128)(2,1)S(1)}, bf16[4,128,256]{2,1,0:T(8,128)(2,1)S(1)}, u32[]{:S(2)}, u32[]{:S(2)}) %collective-permute-start.41) | collective-permute-done | bytes 262176 | tf_op jit(solution)/shard_map/ppermute | solution.py:180
  149.8 7.2 %project_in.5 = (f32[256,768]{1,0:T(8,128)S(1)}, bf16[256,768]{1,0:T(8,128)(2,1)S(1)}) custom-call(bf16[16,7168]{1,0:T(8,128)(2,1)S(1)} %get-tuple-element.21.refs_0_, bf16[16,7168]{1,0:T(8,128)(2,1)} %collective-permute-done.15.refs_1_, bf16[16,7168]{1,0:T(8,128)(2,1)} %collective-permute-done.16.refs_2_, bf16[16,7168]{1,0:T(8,128)(2,1)} %collective-permute-done.17.refs_3_, ...), custom_call_target="tpu_custom_call" | custom-call | flops 2818572288 | bytes 11010048 | tf_op jit(solution)/shard_map/project_in/pallas_call | solution.py:89
  157.8 10.8 %collective-permute-done.31.refs_3_ = bf16[256,768]{1,0:T(8,128)(2,1)S(1)} collective-permute-done((bf16[256,768]{1,0:T(8,128)(2,1)S(1)}, bf16[256,768]{1,0:T(8,128)(2,1)S(1)}, u32[]{:S(2)}, u32[]{:S(2)}) %collective-permute-start.31) | collective-permute-done | bytes 393248 | tf_op jit(solution)/shard_map/ppermute | solution.py:180
  168.5 9.0 %correction.1 = f32[2048,1792]{1,0:T(8,128)} custom-call(s32[16]{0:T(128)S(1)} %get-tuple-element.53.order, s32[16]{0:T(128)S(1)} %get-tuple-element.52.rows, f32[256,1024]{1,0:T(8,128)S(1)} %get-tuple-element.29.refs_0_, f32[256,768]{1,0:T(8,128)S(1)} %get-tuple-element.30.refs_1_, bf16[256,1024]{1,0:T(8,128)(2,1)S(1)} %collective-permute-done.30.refs_2_, ...), custom_call_target="tpu_custom_call" | custom-call | flops 3758096384 | bytes 14680064 | tf_op jit(solution)/shard_map/correction/pallas_call | solution.py:150
  (143 shorter events, 38.1 us)
Async XLA Ops:
  0.0 6.7 %collective-permute-start.32 = (bf16[128,512]{1,0:T(8,128)(2,1)}, bf16[128,512]{1,0:T(8,128)(2,1)S(1)}, u32[]{:S(2)}, u32[]{:S(2)}) collective-permute-start(bf16[128,512]{1,0:T(8,128)(2,1)} %refs_0_.1), channel_id=1, source_target_pairs={{0,16},{16,0},{1,17},{17,1},{2,18},{18,2},{3,19},{19,3},{4,20},{20... | collective-permute-start | bytes 393224 | tf_op jit(solution)/shard_map/ppermute | solution.py:180
  12.9 62.6 %collective-permute-start.33 = (f32[1024,256]{1,0:T(8,128)S(1)}, f32[1024,256]{1,0:T(8,128)S(1)}, u32[]{:S(2)}, u32[]{:S(2)}) collective-permute-start(f32[1024,256]{1,0:T(8,128)S(1)} %get-tuple-element.34), channel_id=1, source_target_pairs={{0,1},{1,0},{2,3},{3,2},{4,5},{5,4},{6,7},{7,6},{8,9},{9,8},{10,11... | collective-permute-start | bytes 3145736 | tf_op jit(solution)/shard_map/ppermute | solution.py:180
  14.1 10.0 %collective-permute-start.20 = (bf16[16,7168]{1,0:T(8,128)(2,1)S(1)}, bf16[16,7168]{1,0:T(8,128)(2,1)S(1)}, u32[]{:S(2)}, u32[]{:S(2)}) collective-permute-start(bf16[16,7168]{1,0:T(8,128)(2,1)S(1)} %get-tuple-element.21.refs_0_), channel_id=1, source_target_pairs={{0,12},{1,13},{2,14},{3,15},{4,0},{5,1},{6,2},{7,3},{8,4},{9,5},{1... | collective-permute-start | bytes 688136 | tf_op jit(solution)/shard_map/ppermute | solution.py:180
  18.0 20.8 %collective-permute-start.18 = (bf16[16,7168]{1,0:T(8,128)(2,1)S(1)}, bf16[16,7168]{1,0:T(8,128)(2,1)}, u32[]{:S(2)}, u32[]{:S(2)}) collective-permute-start(bf16[16,7168]{1,0:T(8,128)(2,1)S(1)} %get-tuple-element.21.refs_0_), channel_id=1, source_target_pairs={{0,8},{1,9},{2,10},{3,11},{4,12},{5,13},{6,14},{7,15},{8,0},{9,1},... | collective-permute-start | bytes 688136 | tf_op jit(solution)/shard_map/ppermute | solution.py:180
  18.0 20.8 %collective-permute-start.16 = (bf16[16,7168]{1,0:T(8,128)(2,1)S(1)}, bf16[16,7168]{1,0:T(8,128)(2,1)}, u32[]{:S(2)}, u32[]{:S(2)}) collective-permute-start(bf16[16,7168]{1,0:T(8,128)(2,1)S(1)} %get-tuple-element.21.refs_0_), channel_id=1, source_target_pairs={{0,4},{1,5},{2,6},{3,7},{4,8},{5,9},{6,10},{7,11},{8,12},{9,13},{1... | collective-permute-start | bytes 688136 | tf_op jit(solution)/shard_map/ppermute | solution.py:180
  19.0 30.6 %collective-permute-start.7 = (bf16[16,7168]{1,0:T(8,128)(2,1)S(1)}, bf16[16,7168]{1,0:T(8,128)(2,1)S(1)}, u32[]{:S(2)}, u32[]{:S(2)}) collective-permute-start(bf16[16,7168]{1,0:T(8,128)(2,1)S(1)} %get-tuple-element.42.refs_0_), channel_id=1, source_target_pairs={{0,1},{1,0},{2,3},{3,2},{4,5},{5,4},{6,7},{7,6},{8,9},{9,8},{10,11... | collective-permute-start | bytes 688136 | tf_op jit(solution)/shard_map/ppermute | solution.py:180
  24.1 28.5 %collective-permute-start.5 = (bf16[16,7168]{1,0:T(8,128)(2,1)S(1)}, bf16[16,7168]{1,0:T(8,128)(2,1)S(1)}, u32[]{:S(2)}, u32[]{:S(2)}) collective-permute-start(bf16[16,7168]{1,0:T(8,128)(2,1)S(1)} %get-tuple-element.42.refs_0_), channel_id=1, source_target_pairs={{0,12},{1,13},{2,14},{3,15},{4,0},{5,1},{6,2},{7,3},{8,4},{9,5},{1... | collective-permute-start | bytes 688136 | tf_op jit(solution)/shard_map/ppermute | solution.py:180
  38.8 19.1 %collective-permute-start.3 = (bf16[16,7168]{1,0:T(8,128)(2,1)S(1)}, bf16[16,7168]{1,0:T(8,128)(2,1)S(1)}, u32[]{:S(2)}, u32[]{:S(2)}) collective-permute-start(bf16[16,7168]{1,0:T(8,128)(2,1)S(1)} %get-tuple-element.42.refs_0_), channel_id=1, source_target_pairs={{0,8},{1,9},{2,10},{3,11},{4,12},{5,13},{6,14},{7,15},{8,0},{9,1},... | collective-permute-start | bytes 688136 | tf_op jit(solution)/shard_map/ppermute | solution.py:180
  38.8 21.3 %collective-permute-start.1 = (bf16[16,7168]{1,0:T(8,128)(2,1)S(1)}, bf16[16,7168]{1,0:T(8,128)(2,1)S(1)}, u32[]{:S(2)}, u32[]{:S(2)}) collective-permute-start(bf16[16,7168]{1,0:T(8,128)(2,1)S(1)} %get-tuple-element.42.refs_0_), channel_id=1, source_target_pairs={{0,4},{1,5},{2,6},{3,7},{4,8},{5,9},{6,10},{7,11},{8,12},{9,13},{1... | collective-permute-start | bytes 688136 | tf_op jit(solution)/shard_map/ppermute | solution.py:180
  50.3 9.8 %collective-permute-start = (bf16[16,7168]{1,0:T(8,128)(2,1)S(1)}, bf16[16,7168]{1,0:T(8,128)(2,1)S(1)}, u32[]{:S(2)}, u32[]{:S(2)}) collective-permute-start(bf16[16,7168]{1,0:T(8,128)(2,1)S(1)} %get-tuple-element.42.refs_0_), channel_id=1, source_target_pairs={{0,2},{1,3},{2,0},{3,1},{4,6},{5,7},{6,4},{7,5},{8,10},{9,11},{10,... | collective-permute-start | bytes 688136 | tf_op jit(solution)/shard_map/ppermute | solution.py:180
  52.6 8.8 %collective-permute-start.13 = (bf16[16,7168]{1,0:T(8,128)(2,1)S(1)}, bf16[16,7168]{1,0:T(8,128)(2,1)S(1)}, u32[]{:S(2)}, u32[]{:S(2)}) collective-permute-start(bf16[16,7168]{1,0:T(8,128)(2,1)S(1)} %collective-permute-done.5.refs_6_), channel_id=1, source_target_pairs={{0,1},{1,0},{2,3},{3,2},{4,5},{5,4},{6,7},{7,6},{8,9},{9,8},{10,11... | collective-permute-start | bytes 688136 | tf_op jit(solution)/shard_map/ppermute | solution.py:180
  57.9 8.5 %collective-permute-start.6 = (bf16[16,7168]{1,0:T(8,128)(2,1)S(1)}, bf16[16,7168]{1,0:T(8,128)(2,1)S(1)}, u32[]{:S(2)}, u32[]{:S(2)}) collective-permute-start(bf16[16,7168]{1,0:T(8,128)(2,1)S(1)} %collective-permute-done.5.refs_6_), channel_id=1, source_target_pairs={{0,2},{1,3},{2,0},{3,1},{4,6},{5,7},{6,4},{7,5},{8,10},{9,11},{10,... | collective-permute-start | bytes 688136 | tf_op jit(solution)/shard_map/ppermute | solution.py:180
  60.1 7.0 %collective-permute-start.11 = (bf16[16,7168]{1,0:T(8,128)(2,1)S(1)}, bf16[16,7168]{1,0:T(8,128)(2,1)S(1)}, u32[]{:S(2)}, u32[]{:S(2)}) collective-permute-start(bf16[16,7168]{1,0:T(8,128)(2,1)S(1)} %collective-permute-done.3.refs_4_), channel_id=1, source_target_pairs={{0,1},{1,0},{2,3},{3,2},{4,5},{5,4},{6,7},{7,6},{8,9},{9,8},{10,11... | collective-permute-start | bytes 688136 | tf_op jit(solution)/shard_map/ppermute | solution.py:180
  60.1 11.2 %collective-permute-start.4 = (bf16[16,7168]{1,0:T(8,128)(2,1)S(1)}, bf16[16,7168]{1,0:T(8,128)(2,1)S(1)}, u32[]{:S(2)}, u32[]{:S(2)}) collective-permute-start(bf16[16,7168]{1,0:T(8,128)(2,1)S(1)} %collective-permute-done.3.refs_4_), channel_id=1, source_target_pairs={{0,2},{1,3},{2,0},{3,1},{4,6},{5,7},{6,4},{7,5},{8,10},{9,11},{10,... | collective-permute-start | bytes 688136 | tf_op jit(solution)/shard_map/ppermute | solution.py:180
  62.0 12.8 %collective-permute-start.2 = (bf16[16,7168]{1,0:T(8,128)(2,1)S(1)}, bf16[16,7168]{1,0:T(8,128)(2,1)S(1)}, u32[]{:S(2)}, u32[]{:S(2)}) collective-permute-start(bf16[16,7168]{1,0:T(8,128)(2,1)S(1)} %collective-permute-done.1.refs_2_), channel_id=1, source_target_pairs={{0,2},{1,3},{2,0},{3,1},{4,6},{5,7},{6,4},{7,5},{8,10},{9,11},{10,... | collective-permute-start | bytes 688136 | tf_op jit(solution)/shard_map/ppermute | solution.py:180
  66.3 13.3 %collective-permute-start.9 = (bf16[16,7168]{1,0:T(8,128)(2,1)S(1)}, bf16[16,7168]{1,0:T(8,128)(2,1)S(1)}, u32[]{:S(2)}, u32[]{:S(2)}) collective-permute-start(bf16[16,7168]{1,0:T(8,128)(2,1)S(1)} %collective-permute-done.1.refs_2_), channel_id=1, source_target_pairs={{0,1},{1,0},{2,3},{3,2},{4,5},{5,4},{6,7},{7,6},{8,9},{9,8},{10,11... | collective-permute-start | bytes 688136 | tf_op jit(solution)/shard_map/ppermute | solution.py:180
  67.7 14.1 %collective-permute-start.8 = (bf16[16,7168]{1,0:T(8,128)(2,1)S(1)}, bf16[16,7168]{1,0:T(8,128)(2,1)S(1)}, u32[]{:S(2)}, u32[]{:S(2)}) collective-permute-start(bf16[16,7168]{1,0:T(8,128)(2,1)S(1)} %collective-permute-done.refs_1_), channel_id=1, source_target_pairs={{0,1},{1,0},{2,3},{3,2},{4,5},{5,4},{6,7},{7,6},{8,9},{9,8},{10,11... | collective-permute-start | bytes 688136 | tf_op jit(solution)/shard_map/ppermute | solution.py:180
  71.2 11.8 %collective-permute-start.14 = (bf16[16,7168]{1,0:T(8,128)(2,1)S(1)}, bf16[16,7168]{1,0:T(8,128)(2,1)S(1)}, u32[]{:S(2)}, u32[]{:S(2)}) collective-permute-start(bf16[16,7168]{1,0:T(8,128)(2,1)S(1)} %collective-permute-done.6.refs_7_), channel_id=1, source_target_pairs={{0,1},{1,0},{2,3},{3,2},{4,5},{5,4},{6,7},{7,6},{8,9},{9,8},{10,11... | collective-permute-start | bytes 688136 | tf_op jit(solution)/shard_map/ppermute | solution.py:180
  74.8 10.5 %collective-permute-start.12 = (bf16[16,7168]{1,0:T(8,128)(2,1)S(1)}, bf16[16,7168]{1,0:T(8,128)(2,1)}, u32[]{:S(2)}, u32[]{:S(2)}) collective-permute-start(bf16[16,7168]{1,0:T(8,128)(2,1)S(1)} %collective-permute-done.4.refs_5_), channel_id=1, source_target_pairs={{0,1},{1,0},{2,3},{3,2},{4,5},{5,4},{6,7},{7,6},{8,9},{9,8},{10,11... | collective-permute-start | bytes 688136 | tf_op jit(solution)/shard_map/ppermute | solution.py:180
  76.5 9.3 %collective-permute-start.10 = (bf16[16,7168]{1,0:T(8,128)(2,1)S(1)}, bf16[16,7168]{1,0:T(8,128)(2,1)}, u32[]{:S(2)}, u32[]{:S(2)}) collective-permute-start(bf16[16,7168]{1,0:T(8,128)(2,1)S(1)} %collective-permute-done.2.refs_3_), channel_id=1, source_target_pairs={{0,1},{1,0},{2,3},{3,2},{4,5},{5,4},{6,7},{7,6},{8,9},{9,8},{10,11... | collective-permute-start | bytes 688136 | tf_op jit(solution)/shard_map/ppermute | solution.py:180
  80.3 33.4 %collective-permute-start.15 = (bf16[16,7168]{1,0:T(8,128)(2,1)S(1)}, bf16[16,7168]{1,0:T(8,128)(2,1)}, u32[]{:S(2)}, u32[]{:S(2)}) collective-permute-start(bf16[16,7168]{1,0:T(8,128)(2,1)S(1)} %get-tuple-element.21.refs_0_), channel_id=1, source_target_pairs={{0,2},{1,3},{2,0},{3,1},{4,6},{5,7},{6,4},{7,5},{8,10},{9,11},{10,... | collective-permute-start | bytes 688136 | tf_op jit(solution)/shard_map/ppermute | solution.py:180
  82.6 31.2 %collective-permute-start.21 = (bf16[16,7168]{1,0:T(8,128)(2,1)S(1)}, bf16[16,7168]{1,0:T(8,128)(2,1)S(1)}, u32[]{:S(2)}, u32[]{:S(2)}) collective-permute-start(bf16[16,7168]{1,0:T(8,128)(2,1)S(1)} %collective-permute-done.20.refs_6_), channel_id=1, source_target_pairs={{0,2},{1,3},{2,0},{3,1},{4,6},{5,7},{6,4},{7,5},{8,10},{9,11},{10,... | collective-permute-start | bytes 688136 | tf_op jit(solution)/shard_map/ppermute | solution.py:180
  83.8 31.2 %collective-permute-start.19 = (bf16[16,7168]{1,0:T(8,128)(2,1)}, bf16[16,7168]{1,0:T(8,128)(2,1)}, u32[]{:S(2)}, u32[]{:S(2)}) collective-permute-start(bf16[16,7168]{1,0:T(8,128)(2,1)} %collective-permute-done.18.refs_4_), channel_id=1, source_target_pairs={{0,2},{1,3},{2,0},{3,1},{4,6},{5,7},{6,4},{7,5},{8,10},{9,11},{10,... | collective-permute-start | bytes 688136 | tf_op jit(solution)/shard_map/ppermute | solution.py:180
  85.3 29.7 %collective-permute-start.17 = (bf16[16,7168]{1,0:T(8,128)(2,1)}, bf16[16,7168]{1,0:T(8,128)(2,1)}, u32[]{:S(2)}, u32[]{:S(2)}) collective-permute-start(bf16[16,7168]{1,0:T(8,128)(2,1)} %collective-permute-done.16.refs_2_), channel_id=1, source_target_pairs={{0,2},{1,3},{2,0},{3,1},{4,6},{5,7},{6,4},{7,5},{8,10},{9,11},{10,... | collective-permute-start | bytes 688136 | tf_op jit(solution)/shard_map/ppermute | solution.py:180
  85.8 31.3 %collective-permute-start.34 = (f32[512,256]{1,0:T(8,128)}, f32[512,256]{1,0:T(8,128)}, u32[]{:S(2)}, u32[]{:S(2)}) collective-permute-start(f32[512,256]{1,0:T(8,128)} %add_bitcast_fusion), channel_id=1, source_target_pairs={{0,2},{1,3},{2,0},{3,1},{4,6},{5,7},{6,4},{7,5},{8,10},{9,11},{10,... | collective-permute-start | bytes 1572872 | tf_op jit(solution)/shard_map/ppermute | solution.py:180
  118.7 15.0 %collective-permute-start.35 = (f32[128,256]{1,0:T(8,128)S(1)}, f32[128,256]{1,0:T(8,128)S(1)}, u32[]{:S(2)}, u32[]{:S(2)}) collective-permute-start(f32[128,256]{1,0:T(8,128)S(1)} %get-tuple-element.39), channel_id=1, source_target_pairs={{0,4},{1,5},{2,6},{3,7},{4,8},{5,9},{6,10},{7,11},{8,12},{9,13},{1... | collective-permute-start | bytes 393224 | tf_op jit(solution)/shard_map/ppermute | solution.py:180
  118.8 14.9 %collective-permute-start.37 = (f32[128,256]{1,0:T(8,128)S(1)}, f32[128,256]{1,0:T(8,128)S(1)}, u32[]{:S(2)}, u32[]{:S(2)}) collective-permute-start(f32[128,256]{1,0:T(8,128)S(1)} %get-tuple-element.40), channel_id=1, source_target_pairs={{0,12},{1,13},{2,14},{3,15},{4,0},{5,1},{6,2},{7,3},{8,4},{9,5},{1... | collective-permute-start | bytes 393224 | tf_op jit(solution)/shard_map/ppermute | solution.py:180
  122.6 11.1 %collective-permute-start.36 = (f32[128,256]{1,0:T(8,128)S(1)}, f32[128,256]{1,0:T(8,128)S(1)}, u32[]{:S(2)}, u32[]{:S(2)}) collective-permute-start(f32[128,256]{1,0:T(8,128)S(1)} %get-tuple-element.41), channel_id=1, source_target_pairs={{0,8},{1,9},{2,10},{3,11},{4,12},{5,13},{6,14},{7,15},{8,0},{9,1},... | collective-permute-start | bytes 393224 | tf_op jit(solution)/shard_map/ppermute | solution.py:180
  132.1 36.4 %collective-permute-start.30 = (bf16[256,1024]{1,0:T(8,128)(2,1)S(1)}, bf16[256,1024]{1,0:T(8,128)(2,1)S(1)}, u32[]{:S(2)}, u32[]{:S(2)}) collective-permute-start(bf16[256,1024]{1,0:T(8,128)(2,1)S(1)} %get-tuple-element.31), channel_id=1, source_target_pairs={{0,16},{16,0},{1,17},{17,1},{2,18},{18,2},{3,19},{19,3},{4,20},{20... | collective-permute-start | bytes 1572872 | tf_op jit(solution)/shard_map/ppermute | solution.py:180
  142.9 6.7 %collective-permute-start.41 = (bf16[4,128,256]{2,1,0:T(8,128)(2,1)S(1)}, bf16[4,128,256]{2,1,0:T(8,128)(2,1)S(1)}, u32[]{:S(2)}, u32[]{:S(2)}) collective-permute-start(bf16[4,128,256]{2,1,0:T(8,128)(2,1)S(1)} %pad_maximum_fusion), channel_id=1, source_target_pairs={{0,2},{1,3},{2,0},{3,1},{4,6},{5,7},{6,4},{7,5},{8,10},{9,11},{10,... | collective-permute-start | bytes 786440 | tf_op jit(solution)/shard_map/ppermute | solution.py:180
  149.7 8.0 %collective-permute-start.42 = (bf16[8,128,256]{2,1,0:T(8,128)(2,1)S(1)}, bf16[8,128,256]{2,1,0:T(8,128)(2,1)S(1)}, u32[]{:S(2)}, u32[]{:S(2)}) collective-permute-start(bf16[8,128,256]{2,1,0:T(8,128)(2,1)S(1)} %get-tuple-element.44), channel_id=1, source_target_pairs={{0,1},{1,0},{2,3},{3,2},{4,5},{5,4},{6,7},{7,6},{8,9},{9,8},{10,11... | collective-permute-start | bytes 1572872 | tf_op jit(solution)/shard_map/ppermute | solution.py:180
  157.0 11.5 %collective-permute-start.31 = (bf16[256,768]{1,0:T(8,128)(2,1)S(1)}, bf16[256,768]{1,0:T(8,128)(2,1)S(1)}, u32[]{:S(2)}, u32[]{:S(2)}) collective-permute-start(bf16[256,768]{1,0:T(8,128)(2,1)S(1)} %get-tuple-element.32), channel_id=1, source_target_pairs={{0,16},{16,0},{1,17},{17,1},{2,18},{18,2},{3,19},{19,3},{4,20},{20... | collective-permute-start | bytes 1179656 | tf_op jit(solution)/shard_map/ppermute | solution.py:180
  (46 other events, 120.0 us)
